TPU v7x, 32 devices: a whole 2x2x4 slice. The times are simulated.
32 devices in a mesh: row: 2 (over y), col: 8 (over z, x), rep: 2 (over core).
Axes of the slice: x: 2, y: 2, z: 4, core: 2. Of those that a mesh axis runs over, the one named last changes fastest.
Arguments:
- gain: float32 [48, 8, 128, 128], P(('row', 'col'), 'rep'), as said below
- coupled_columns: int32 [48, 8], P(('row', 'col')), may hold values from 0 to 47, as said below
- solution: float32 [6144, 512], P(('row', 'col')), may hold values from -6 to 6
- residual: float32 [6144, 512], P(('row', 'col')), may hold values from -6 to 6
- direction: float32 [6144, 512], P(('row', 'col')), may hold values from -6 to 6
Outputs:
- solution_next: float32 [6144, 512], P(('row', 'col'))
- residual_next: float32 [6144, 512], P(('row', 'col'))
- direction_next: float32 [6144, 512], P(('row', 'col'))
Inputs may be any that keep to these rules, and one draw needn't show every extreme that they name: `coupled_columns`: each block row i names first its coupled block columns in ascending order (always i - 1, i, i + 1 where inside 0 to 47, some of i - 3, i - 2, i + 2, i + 3, the coupling being symmetric), at most 7 of them, and then fills the remaining slots with i itself; every named column is within 3 of i. The gain matrix assembled from its blocks is symmetric; padding slots hold zero blocks; each diagonal entry exceeds the sum of the absolute values of the other entries of its row by exactly 1.
All inputs are finite; a program needn't handle non-finite values.
Results may differ from a plain program's by a relative error of at most 0.000061.
Values sent between devices are 32-bit elements; how exact they have to be, the bound alone decides.
A program may use at most 64 MiB of HBM per device.

v0:
```python
import jax
import jax.numpy as jnp
from jax import lax
from jax.sharding import PartitionSpec as P

BLK = 128
reach_blocks = 3


def extended_2(block, sides, width):
    for axis, dim in sides:
        count = lax.axis_size(axis)
        forward = [(i, i + 1) for i in range(count - 1)]
        backward = [(target, source) for source, target in forward]
        low = lax.ppermute(
            lax.slice_in_dim(block, block.shape[dim] - width, None, axis=dim), axis, forward
        )
        high = lax.ppermute(lax.slice_in_dim(block, 0, width, axis=dim), axis, backward)
        block = jnp.concatenate([low, block, high], axis=dim)
    return block


def per_device(gain, coupled_columns, solution, residual, direction):
    row_blocks = coupled_columns.shape[0]
    snapshots = direction.shape[1]
    first_block = lax.axis_index(("row", "col")) * row_blocks
    extended = extended_2(direction, ((("row", "col"), 0),), reach_blocks * BLK)
    segments = extended.reshape(row_blocks + 2 * reach_blocks, BLK, snapshots)
    half_slots = gain.shape[1]
    own_columns = lax.dynamic_slice_in_dim(
        coupled_columns, lax.axis_index("rep") * half_slots, half_slots, 1
    )
    local_index = own_columns - first_block + reach_blocks
    picked = segments[local_index]
    product = jnp.einsum(
        "rkab,rkbs->ras",
        gain,
        picked,
        precision=lax.Precision.HIGHEST,
        preferred_element_type=jnp.float32,
    )
    image = lax.psum(product.reshape(row_blocks * BLK, snapshots), "rep")
    norm_old, curvature, crossing, image_square = lax.psum(
        (
            jnp.sum(residual * residual, axis=0),
            jnp.sum(direction * image, axis=0),
            jnp.sum(residual * image, axis=0),
            jnp.sum(image * image, axis=0),
        ),
        ("row", "col"),
    )
    step_size = norm_old / curvature
    solution_next = solution + step_size * direction
    residual_next = residual - step_size * image
    norm_new = norm_old - 2.0 * step_size * crossing + step_size * step_size * image_square
    direction_next = residual_next + norm_new / norm_old * direction
    return (solution_next, residual_next, direction_next)


def solution(mesh):
    return jax.shard_map(
        per_device,
        mesh=mesh,
        in_specs=(
            P(("row", "col"), "rep", None, None),
            P(("row", "col"), None),
            P(("row", "col"), None),
            P(("row", "col"), None),
            P(("row", "col"), None),
        ),
        out_specs=(P(("row", "col"), None), P(("row", "col"), None), P(("row", "col"), None)),
        check_vma=False,
    )
```

profile of v0, /device:TPU:0, one launch (start us, length us, event | category | flops | bytes accessed | tf_op | source)
XLA Modules:
  0.0 132.4 jit_solution(13395826707546090617)
XLA Ops:
  7.2 0.0 copy-start
  7.2 0.0 all-reduce.3.cloned.1.call-start
  7.2 1.4 %collective-permute-start.1 = (f32[384,512]{1,0:T(8,128)}, f32[384,512]{1,0:T(8,128)S(1)}, u32[]{:S(2)}, u32[]{:S(2)}) collective-permute-start(f32[384,512]{1,0:T(8,128)} %param.9), channel_id=1, source_target_pairs={{2,0},{4,2},{6,4},{8,6},{10,8},{12,10},{14,12},{16,14},{18,16},{20... | collective-permute-start | bytes 2359304 | tf_op jit(solution)/shard_map/ppermute | solution.py:18
  8.7 6.4 %collective-permute-start = (f32[384,512]{1,0:T(8,128)}, f32[384,512]{1,0:T(8,128)}, u32[]{:S(2)}, u32[]{:S(2)}) collective-permute-start(f32[384,512]{1,0:T(8,128)} %param.9), channel_id=1, source_target_pairs={{0,2},{2,4},{4,6},{6,8},{8,10},{10,12},{12,14},{14,16},{16,18},{18... | collective-permute-start | bytes 2359304 | tf_op jit(solution)/shard_map/ppermute | solution.py:15
  15.0 0.8 compare_select_fusion
  15.8 0.1 reshape.18
  15.9 30.9 %collective-permute-done.1 = f32[384,512]{1,0:T(8,128)S(1)} collective-permute-done((f32[384,512]{1,0:T(8,128)}, f32[384,512]{1,0:T(8,128)S(1)}, u32[]{:S(2)}, u32[]{:S(2)}) %collective-permute-start.1) | collective-permute-done | bytes 786464 | tf_op jit(solution)/shard_map/ppermute | solution.py:18
  46.8 0.0 copy-start.4
  46.8 0.9 copy-done.4
  47.7 0.0 collective-permute-done
  47.7 1.8 %pad_maximum_fusion = f32[1152,512]{1,0:T(8,128)S(1)} fusion(f32[384,512]{1,0:T(8,128)} %copy-done.4, f32[384,512]{1,0:T(8,128)} %param.9, f32[384,512]{1,0:T(8,128)} %collective-permute-done), kind=kLoop, calls=%fused_computation.1 | loop fusion | flops 1179648 | bytes 4718592 | tf_op jit(solution)/shard_map/concatenate | solution.py:19
  49.5 2.4 %gather_fusion = f32[12,128,512]{2,1,0:T(8,128)} fusion(f32[9,128,512]{2,1,0:T(8,128)S(1)} %bitcast.10, s32[1024]{0:T(1024)S(1)} %pad_clamp_fusion), kind=kCustom, calls=%fused_computation | custom fusion | bytes 6291504 | tf_op jit(solution)/shard_map/gather | solution.py:34
  51.9 0.0 copy-start.1
  51.9 0.0 copy-start.2
  51.9 0.0 copy-done
  52.0 4.8 %fusion = f32[3,512,128,1]{1,2,3,0:T(8,128)} fusion(f32[3,4,128,512]{3,2,1,0:T(8,128)} %bitcast.11, f32[3,4,128,128]{3,2,1,0:T(8,128)S(1)} %copy-done), kind=kOutput, calls=%fused_computation.12 | convolution fusion | flops 1207959552 | bytes 4718592 | tf_op jit(solution)/shard_map/rkab,rkbs->ras/dot_general | solution.py:35
  56.7 0.0 all-reduce.3.cloned.1.call-update
  56.7 22.1 %all-reduce.3.cloned.1.call-done = f32[384,512]{1,0:T(8,128)} async-done(((f32[384,512]{1,0:T(8,128)}), f32[384,512]{1,0:T(8,128)}) %all-reduce.3.cloned.1.call-update) | async-done | bytes 786448 | tf_op jit(solution)/shard_map/psum | solution.py:42
  78.8 0.0 copy-done.1
  78.8 0.0 copy-done.2
  78.8 1.4 %multiply_reduce_fusion.1 = (f32[512]{0:T(512)S(1)}, f32[512]{0:T(512)S(1)}, f32[512]{0:T(512)S(1)}, f32[512]{0:T(512)S(1)}) fusion(f32[384,512]{1,0:T(8,128)S(1)} %copy-done.2, f32[384,512]{1,0:T(8,128)} %all-reduce.3.cloned.1.call-done, f32[384,512]{1,0:T(8,128)S(1)} %copy-done.1), kind=kLoop, calls=%fused_computation.4 | loop fusion | flops 1570816 | bytes 2367488 | tf_op jit(solution)/shard_map/reduce_sum | solution.py:47
  80.2 42.5 %all-reduce = (f32[512]{0:T(512)S(1)}, f32[512]{0:T(512)S(1)}, f32[512]{0:T(512)S(1)}, f32[512]{0:T(512)S(1)}) all-reduce(f32[512]{0:T(512)S(1)} %get-tuple-element.6, f32[512]{0:T(512)S(1)} %get-tuple-element.5, f32[512]{0:T(512)S(1)} %get-tuple-element.4, ...), channel_id=1, replica_groups=mesh['row'=2,'col'=8,'rep'=2] {'row','col'}, use_global_device_ids=true, to_apply=%region_1.0 | all-reduce | flops 2048 | bytes 16384 | tf_op jit(solution)/shard_map/psum | solution.py:43
  122.8 0.0 copy-done.3
  122.8 2.8 %multiply_add_fusion = (f32[384,512]{1,0:T(8,128)}, f32[384,512]{1,0:T(8,128)}, f32[384,512]{1,0:T(8,128)}) fusion(f32[384,512]{1,0:T(8,128)S(1)} %copy-done.1, f32[512]{0:T(512)S(1)} %get-tuple-element.13, f32[384,512]{1,0:T(8,128)S(1)} %copy-done.2, f32[384,512]{1,0:T(8,128)} %all-reduce.3.cloned.1.call-done, f32[512]{0:T(512)S(1)} %get-tuple-element.14, ...), kind=kLoop, calls=%fused_computation.2 | loop fusion | flops 1179648 | bytes 5509120 | tf_op jit(solution)/shard_map/add | solution.py:56
  (3 shorter events, 0.0 us)
Async XLA Ops:
  7.2 44.8 %copy-start = (f32[3,4,128,128]{3,2,1,0:T(8,128)S(1)}, f32[3,4,128,128]{3,2,1,0:T(8,128)}, u32[]{:S(2)}) copy-start(f32[3,4,128,128]{3,2,1,0:T(8,128)} %param.5) | copy-start | bytes 2359300
  7.2 71.6 %all-reduce.3.cloned.1.call-start = ((), (), s32[]{:S(2)}) async-start(), calls=%async_computation | async-start | bytes 1572864 | tf_op jit(solution)/shard_map/psum | solution.py:42
  7.2 39.6 %collective-permute-start.1 = (f32[384,512]{1,0:T(8,128)}, f32[384,512]{1,0:T(8,128)S(1)}, u32[]{:S(2)}, u32[]{:S(2)}) collective-permute-start(f32[384,512]{1,0:T(8,128)} %param.9), channel_id=1, source_target_pairs={{2,0},{4,2},{6,4},{8,6},{10,8},{12,10},{14,12},{16,14},{18,16},{20... | collective-permute-start | bytes 2359304 | tf_op jit(solution)/shard_map/ppermute | solution.py:18
  8.7 39.1 %collective-permute-start = (f32[384,512]{1,0:T(8,128)}, f32[384,512]{1,0:T(8,128)}, u32[]{:S(2)}, u32[]{:S(2)}) collective-permute-start(f32[384,512]{1,0:T(8,128)} %param.9), channel_id=1, source_target_pairs={{0,2},{2,4},{4,6},{6,8},{8,10},{10,12},{12,14},{14,16},{16,18},{18... | collective-permute-start | bytes 2359304 | tf_op jit(solution)/shard_map/ppermute | solution.py:15
  46.8 0.9 copy-start.4
  51.9 26.9 %copy-start.1 = (f32[384,512]{1,0:T(8,128)S(1)}, f32[384,512]{1,0:T(8,128)}, u32[]{:S(2)}) copy-start(f32[384,512]{1,0:T(8,128)} %param.9) | copy-start | bytes 2359300
  51.9 26.9 %copy-start.2 = (f32[384,512]{1,0:T(8,128)S(1)}, f32[384,512]{1,0:T(8,128)}, u32[]{:S(2)}) copy-start(f32[384,512]{1,0:T(8,128)} %param.8) | copy-start | bytes 2359300
  52.0 70.8 %copy-start.3 = (f32[384,512]{1,0:T(8,128)S(1)}, f32[384,512]{1,0:T(8,128)}, u32[]{:S(2)}) copy-start(f32[384,512]{1,0:T(8,128)} %param.7) | copy-start | bytes 2359300
Sparse Core Ops, SparseCore 0:
  56.9 21.8 all-reduce.2
where the time goes:
time: 133 us; the launch traced here: 132 us
  waiting for transfers between devices  53 us (40%)
  blocking collectives  42.5 us (32%)
  between operations  14.1 us (11%)
  starting transfers between devices  7.85 us (6%)
  other arithmetic  6.84 us (5%)
  matrix products  4.76 us (4%)
  local copies, waits for them, and re-layouts  3.4 us (3%)
    psum x1, blocking collectives, per_device(): lax.psum((jnp.sum(residual * residual, axis=0), jnp.sum(direction * image...  42.5 us
    ppermute x1, waiting for transfers between devices, extended_2(): lax.ppermute(lax.slice_in_dim(block, 0, width, axis=dim), axis, backward)  30.9 us
    psum x1, waiting for transfers between devices, per_device(): image = lax.psum(product.reshape(row_blocks * BLK, snapshots), 'rep')  22.1 us
    ppermute x1, starting transfers between devices, extended_2(): lax.ppermute(lax.slice_in_dim(block, block.shape[dim] - width, None, axis...  6.39 us
    dot_general x1, matrix products, per_device(): jnp.einsum('rkab,rkbs->ras', gain, picked, precision=lax.Precision.HIGHES...  4.76 us
    add x1, other arithmetic, per_device(): direction_next = residual_next + norm_new / norm_old * direction  2.82 us
  transfers between devices with their start and end apart: 3, of which 2 were waited for; matrix products, arithmetic and copies ran while one was open for 1% of the time, Pallas kernels for 0%

commit v1 on v0

--- a/solution.py
+++ b/solution.py
@@ -39,7 +39,7 @@
         precision=lax.Precision.HIGHEST,
         preferred_element_type=jnp.float32,
     )
-    image = lax.psum(product.reshape(row_blocks * BLK, snapshots), "rep")
+    image = jnp.sum(lax.all_gather(product.reshape(row_blocks * BLK, snapshots), "rep"), axis=0)
     norm_old, curvature, crossing, image_square = lax.psum(
         (
             jnp.sum(residual * residual, axis=0),

time: 133 us -> 124 us (0.932)
  waiting for transfers between devices: 53 us -> 43.8 us
    psum x1 -> x0, waiting for transfers between devices: 22.1 us -> none  [per_device(): image = lax.psum(product.reshape(row_blocks * BLK, snapshots), 'rep')]
    all_gather x0 -> x1, waiting for transfers between devices: none -> 12.9 us  [per_device(): lax.all_gather(product.reshape(row_blocks * BLK, snapshots), 'rep')]
    reduce_sum x0 -> x1, other arithmetic: none -> 1.62 us  [per_device(): jnp.sum(lax.all_gather(product.reshape(row_blocks * BLK, snapshots), 'rep...]
where the time goes in v1:
time: 124 us
  waiting for transfers between devices  43.8 us (35%)
  blocking collectives  42.5 us (34%)
  between operations  14.1 us (11%)
  starting transfers between devices  7.85 us (6%)
  other arithmetic  7.33 us (6%)
  matrix products  4.61 us (4%)
  local copies, waits for them, and re-layouts  3.4 us (3%)
    psum x1, blocking collectives, per_device(): lax.psum((jnp.sum(residual * residual, axis=0), jnp.sum(direction * image...  42.5 us
    ppermute x1, waiting for transfers between devices, extended_2(): lax.ppermute(lax.slice_in_dim(block, 0, width, axis=dim), axis, backward)  30.9 us
    all_gather x1, waiting for transfers between devices, per_device(): lax.all_gather(product.reshape(row_blocks * BLK, snapshots), 'rep')  12.9 us
    ppermute x1, starting transfers between devices, extended_2(): lax.ppermute(lax.slice_in_dim(block, block.shape[dim] - width, None, axis...  6.39 us
    dot_general x1, matrix products, per_device(): jnp.einsum('rkab,rkbs->ras', gain, picked, precision=lax.Precision.HIGHES...  4.61 us
    add x1, other arithmetic, per_device(): direction_next = residual_next + norm_new / norm_old * direction  2.81 us
  transfers between devices with their start and end apart: 3, of which 2 were waited for; matrix products, arithmetic and copies ran while one was open for 1% of the time, Pallas kernels for 0%

profile of v1, /device:TPU:0, one launch (start us, length us, event | category | flops | bytes accessed | tf_op | source)
XLA Modules:
  0.0 123.6 jit_solution(11384302643800708253)
XLA Ops:
  7.2 0.0 copy-start
  7.2 0.0 all-gather.2.cloned.1.call-start
  7.2 1.4 %collective-permute-start.1 = (f32[384,512]{1,0:T(8,128)}, f32[384,512]{1,0:T(8,128)S(1)}, u32[]{:S(2)}, u32[]{:S(2)}) collective-permute-start(f32[384,512]{1,0:T(8,128)} %param.9), channel_id=1, source_target_pairs={{2,0},{4,2},{6,4},{8,6},{10,8},{12,10},{14,12},{16,14},{18,16},{20... | collective-permute-start | bytes 2359304 | tf_op jit(solution)/shard_map/ppermute | solution.py:18
  8.7 6.4 %collective-permute-start = (f32[384,512]{1,0:T(8,128)}, f32[384,512]{1,0:T(8,128)}, u32[]{:S(2)}, u32[]{:S(2)}) collective-permute-start(f32[384,512]{1,0:T(8,128)} %param.9), channel_id=1, source_target_pairs={{0,2},{2,4},{4,6},{6,8},{8,10},{10,12},{12,14},{14,16},{16,18},{18... | collective-permute-start | bytes 2359304 | tf_op jit(solution)/shard_map/ppermute | solution.py:15
  15.0 0.8 compare_select_fusion
  15.8 0.1 reshape.14
  15.9 30.9 %collective-permute-done.1 = f32[384,512]{1,0:T(8,128)S(1)} collective-permute-done((f32[384,512]{1,0:T(8,128)}, f32[384,512]{1,0:T(8,128)S(1)}, u32[]{:S(2)}, u32[]{:S(2)}) %collective-permute-start.1) | collective-permute-done | bytes 786464 | tf_op jit(solution)/shard_map/ppermute | solution.py:18
  46.8 0.0 copy-start.3
  46.8 0.9 copy-done.3
  47.7 0.0 collective-permute-done
  47.7 1.8 %pad_maximum_fusion = f32[1152,512]{1,0:T(8,128)S(1)} fusion(f32[384,512]{1,0:T(8,128)} %copy-done.3, f32[384,512]{1,0:T(8,128)} %param.9, f32[384,512]{1,0:T(8,128)} %collective-permute-done), kind=kLoop, calls=%fused_computation.1 | loop fusion | flops 1179648 | bytes 4718592 | tf_op jit(solution)/shard_map/concatenate | solution.py:19
  49.5 2.4 %gather_fusion = f32[12,128,512]{2,1,0:T(8,128)} fusion(f32[9,128,512]{2,1,0:T(8,128)S(1)} %bitcast.10, s32[1024]{0:T(1024)S(1)} %pad_clamp_fusion), kind=kCustom, calls=%fused_computation | custom fusion | bytes 6291504 | tf_op jit(solution)/shard_map/gather | solution.py:34
  51.9 0.0 copy-done
  51.9 4.6 %fusion = f32[3,512,128,1]{1,2,3,0:T(8,128)} fusion(f32[3,4,128,512]{3,2,1,0:T(8,128)} %bitcast.11, f32[3,4,128,128]{3,2,1,0:T(8,128)S(1)} %copy-done), kind=kOutput, calls=%fused_computation.12 | convolution fusion | flops 1207959552 | bytes 4718592 | tf_op jit(solution)/shard_map/rkab,rkbs->ras/dot_general | solution.py:35
  56.6 0.0 copy-start.1
  56.6 0.0 copy-start.2
  56.6 0.0 all-gather.2.cloned.1.call-update
  56.6 12.9 %all-gather.2.cloned.1.call-done = f32[2,384,512]{2,1,0:T(8,128)} async-done(((f32[1,384,512]{2,1,0:T(8,128)}), f32[2,384,512]{2,1,0:T(8,128)}) %all-gather.2.cloned.1.call-update) | async-done | bytes 1572880 | tf_op jit(solution)/shard_map/all_gather | solution.py:42
  69.5 1.6 %reduce_sum.46 = f32[384,512]{1,0:T(8,128)S(1)} reduce(f32[2,384,512]{2,1,0:T(8,128)} %all-gather.2.cloned.1.call-done, f32[]{:T(128)} %constant.10.clone.1), dimensions={0}, to_apply=%region_2.0 | reduce | flops 196608 | bytes 2359300 | tf_op jit(solution)/shard_map/reduce_sum | solution.py:42
  71.1 0.0 copy-done.1
  71.1 0.0 copy-done.2
  71.1 0.3 multiply_reduce_fusion.1
  71.4 42.5 %all-reduce = (f32[512]{0:T(512)S(1)}, f32[512]{0:T(512)S(1)}, f32[512]{0:T(512)S(1)}, f32[512]{0:T(512)S(1)}) all-reduce(f32[512]{0:T(512)S(1)} %get-tuple-element.6, f32[512]{0:T(512)S(1)} %get-tuple-element.5, f32[512]{0:T(512)S(1)} %get-tuple-element.4, ...), channel_id=1, replica_groups=mesh['row'=2,'col'=8,'rep'=2] {'row','col'}, use_global_device_ids=true, to_apply=%region_1.0 | all-reduce | flops 2048 | bytes 16384 | tf_op jit(solution)/shard_map/psum | solution.py:43
  113.9 2.8 %multiply_add_fusion = (f32[384,512]{1,0:T(8,128)}, f32[384,512]{1,0:T(8,128)}, f32[384,512]{1,0:T(8,128)}) fusion(f32[384,512]{1,0:T(8,128)S(1)} %copy-done.1, f32[512]{0:T(512)S(1)} %get-tuple-element.13, f32[384,512]{1,0:T(8,128)S(1)} %copy-done.2, f32[384,512]{1,0:T(8,128)S(1)} %reduce_sum.46, f32[512]{0:T(512)S(1)} %get-tuple-element.14, f32[384,512]{1,0:T(8,128)} %param.7), kind=kLoop, calls=%fused_computation.2 | loop fusion | flops 1179648 | bytes 5509120 | tf_op jit(solution)/shard_map/add | solution.py:56
  (2 shorter events, 0.0 us)
Async XLA Ops:
  7.2 44.8 %copy-start = (f32[3,4,128,128]{3,2,1,0:T(8,128)S(1)}, f32[3,4,128,128]{3,2,1,0:T(8,128)}, u32[]{:S(2)}) copy-start(f32[3,4,128,128]{3,2,1,0:T(8,128)} %param.5) | copy-start | bytes 2359300
  7.2 62.3 %all-gather.2.cloned.1.call-start = ((), (), s32[]{:S(2)}) async-start(), calls=%async_computation | async-start | bytes 2359296 | tf_op jit(solution)/shard_map/all_gather | solution.py:42
  7.2 39.6 %collective-permute-start.1 = (f32[384,512]{1,0:T(8,128)}, f32[384,512]{1,0:T(8,128)S(1)}, u32[]{:S(2)}, u32[]{:S(2)}) collective-permute-start(f32[384,512]{1,0:T(8,128)} %param.9), channel_id=1, source_target_pairs={{2,0},{4,2},{6,4},{8,6},{10,8},{12,10},{14,12},{16,14},{18,16},{20... | collective-permute-start | bytes 2359304 | tf_op jit(solution)/shard_map/ppermute | solution.py:18
  8.7 39.1 %collective-permute-start = (f32[384,512]{1,0:T(8,128)}, f32[384,512]{1,0:T(8,128)}, u32[]{:S(2)}, u32[]{:S(2)}) collective-permute-start(f32[384,512]{1,0:T(8,128)} %param.9), channel_id=1, source_target_pairs={{0,2},{2,4},{4,6},{6,8},{8,10},{10,12},{12,14},{14,16},{16,18},{18... | collective-permute-start | bytes 2359304 | tf_op jit(solution)/shard_map/ppermute | solution.py:15
  46.8 0.9 copy-start.3
  56.6 14.5 %copy-start.1 = (f32[384,512]{1,0:T(8,128)S(1)}, f32[384,512]{1,0:T(8,128)}, u32[]{:S(2)}) copy-start(f32[384,512]{1,0:T(8,128)} %param.9) | copy-start | bytes 2359300
  56.6 14.6 %copy-start.2 = (f32[384,512]{1,0:T(8,128)S(1)}, f32[384,512]{1,0:T(8,128)}, u32[]{:S(2)}) copy-start(f32[384,512]{1,0:T(8,128)} %param.8) | copy-start | bytes 2359300
Sparse Core Ops, SparseCore 0:
  56.7 12.7 all-gather.1
